TPU v7x, 32 devices: a whole 2x2x4 slice. The times are simulated.
32 devices in a mesh: dp: 4 (over y, x), tp: 8 (over z, core).
Axes of the slice: x: 2, y: 2, z: 4, core: 2. Of those that a mesh axis runs over, the one named last changes fastest.
Arguments:
- proj_in: bfloat16 [1, 4096, 8192], P(None, 'dp', 'tp'), may hold values from -6 to 6
- kv_grad: bfloat16 [1, 4096, 2048], P(None, ('dp', 'tp')), may hold values from -0.1796875 to 0.1796875
- normed: bfloat16 [1, 4096, 8192], P(None, ('dp', 'tp')), may hold values from -6 to 6
- norm_grad: bfloat16 [1, 4096, 8192], P(None, ('dp', 'tp')), may hold values from -0.6 to 0.6
- first_moment: float32 [1, 8192, 2048], P(None, 'tp', 'dp'), may hold values from -0.6 to 0.6
- second_moment: float32 [1, 8192, 2048], P(None, 'tp', 'dp'), may hold values from 0.002 to 0.02
Outputs:
- new_first: float32 [1, 8192, 2048], P(None, 'tp', 'dp')
- new_second: float32 [1, 8192, 2048], P(None, 'tp', 'dp')
- adam_step: float32 [1, 8192, 2048], P(None, 'tp', 'dp')
- gain_grad: float32 [1, 8192], replicated
All inputs are finite; a program needn't handle non-finite values.
Results may differ from a plain program's by a relative error of at most 0.0003.
Values may be sent and summed in bfloat16 or wider, within the bound.
A program may use at most 128 MiB of HBM per device.

v0:
```python
import functools

import jax
import jax.numpy as jnp
from jax import lax
from jax.experimental import pallas as pl
from jax.experimental.pallas import tpu as pltpu
from jax.sharding import PartitionSpec as P

beta_one = 0.9
beta_two = 0.95
correct_one = 0.19
correct_two = 0.0975
epsilon = 1e-08
PIECES = 4
HEADS = 6


def adam_update(mean_grad, first_old, second_old):
    new_first = beta_one * first_old + (1.0 - beta_one) * mean_grad
    new_second = beta_two * second_old + (1.0 - beta_two) * mean_grad * mean_grad
    update = new_first / correct_one / (jnp.sqrt(new_second / correct_two) + epsilon)
    return (new_first, new_second, update)


def kernel(
    n_dp, n_tp, x_hbm, g_hbm, a_hbm, b_hbm, sum_ref, gain_ref,
    xs, kv, a_buf, b_buf, gain_tp, gain_dp,
    local_sem, x_send, x_recv, a2a_send, a2a_recv,
    up_send, up_recv, down_send, down_recv, pair_send, pair_recv,
    gt_send, gt_recv, gd_send, gd_recv,
):
    dp = lax.axis_index("dp")
    tp = lax.axis_index("tp")
    z = tp // 2
    core = tp % 2
    n_z = n_tp // 2
    rows = g_hbm.shape[0]
    cols = kv.shape[2]
    tokens = x_hbm.shape[0]
    piece = tokens // PIECES

    def dp_peer(o):
        return jnp.bitwise_xor(dp, o)

    def tp_peer(o):
        return lax.rem(tp + o, n_tp)

    locals_ = [
        pltpu.make_async_copy(a_hbm, a_buf, local_sem.at[0]),
        pltpu.make_async_copy(b_hbm, b_buf, local_sem.at[1]),
        pltpu.make_async_copy(
            g_hbm.at[:, pl.ds(pl.multiple_of(dp * cols, cols), cols)],
            kv.at[dp, pl.ds(pl.multiple_of(tp * rows, rows), rows), :],
            local_sem.at[2],
        ),
        pltpu.make_async_copy(x_hbm, xs.at[dp], local_sem.at[3]),
    ]
    for copy in locals_:
        copy.start()

    barrier = pltpu.get_barrier_semaphore()
    for o in range(1, n_dp):
        pl.semaphore_signal(barrier, inc=1, device_id={"dp": dp_peer(o)}, device_id_type=pl.DeviceIdType.MESH)
    for o in range(1, n_tp):
        pl.semaphore_signal(barrier, inc=1, device_id={"tp": tp_peer(o)}, device_id_type=pl.DeviceIdType.MESH)
    pl.semaphore_wait(barrier, n_dp - 1 + n_tp - 1)

    sent = []

    def remote(src, dst, send, recv, where):
        return pltpu.make_async_remote_copy(
            src_ref=src, dst_ref=dst, send_sem=send, recv_sem=recv,
            device_id=where, device_id_type=pl.DeviceIdType.MESH,
        )

    my_rows = pl.ds(pl.multiple_of(tp * rows, rows), rows)
    a2a = []
    for o in range(1, n_dp):
        peer = dp_peer(o)
        copy = remote(
            g_hbm.at[:, pl.ds(pl.multiple_of(peer * cols, cols), cols)],
            kv.at[dp, my_rows, :], a2a_send.at[o], a2a_recv.at[o], {"dp": peer},
        )
        copy.start()
        a2a.append(copy)
        sent.append(copy)

    def x_copy(src, origin, c, o_recv, o_to, send):
        part = pl.ds(c * piece, piece)
        return remote(
            src.at[part, :], xs.at[origin, part, :], send, x_recv.at[o_recv, c],
            {"dp": dp_peer(o_to)},
        )

    square = n_dp == 4
    orders = {o: list(range(PIECES)) for o in range(1, n_dp)}
    half = PIECES // 2
    if square:
        orders[2] = list(range(half, PIECES)) + list(range(half))
        orders[3] = []

    def send_own(i):
        for o in range(1, n_dp):
            if i < len(orders[o]):
                c = orders[o][i]
                copy = x_copy(x_hbm, dp, c, o, o, x_send.at[o, c])
                copy.start()
                sent.append(copy)

    def got(o, c):
        x_copy(xs.at[dp_peer(o)], dp_peer(o), c, o, o, x_send.at[o, c]).wait_recv()

    def forward(i):
        for o, o_to in ((1, 2), (2, 1)):
            c = orders[o][i]
            got(o, c)
            copy = x_copy(xs.at[dp_peer(o)], dp_peer(o), c, 3, o_to, x_send.at[3, c])
            copy.start()
            sent.append(copy)

    send_own(0)
    send_own(1)

    locals_[0].wait()
    locals_[1].wait()
    wide = gain_tp.shape[2]
    lines = gain_tp.shape[1]
    for j in range(lines):
        s = pl.ds(j * wide, wide)
        products = a_buf[:, s].astype(jnp.float32) * b_buf[:, s].astype(jnp.float32)
        gain_tp[tp, pl.ds(j, 1), :] = jnp.sum(products, axis=0, keepdims=True)
    tp_copies = []
    for o in range(1, n_tp):
        copy = remote(gain_tp.at[tp], gain_tp.at[tp], gt_send.at[o], gt_recv.at[o], {"tp": tp_peer(o)})
        copy.start()
        sent.append(copy)
        tp_copies.append(copy)

    def block(b, c):
        return kv.at[:, pl.ds(pl.multiple_of((2 * b + c) * rows, rows), rows), :]

    other = 2 * z + 1 - core

    def to_pair(b):
        return remote(block(b, core), block(b, core), pair_send.at[b], pair_recv.at[b], {"tp": other})

    def up(s):
        b = z - s + 1
        return remote(block(b, core), block(b, core), up_send.at[s], up_recv.at[s], {"tp": tp + 2})

    def down(s):
        b = z + s - 1
        return remote(block(b, core), block(b, core), down_send.at[s], down_recv.at[s], {"tp": tp - 2})

    def up_got(s):
        b = z - s
        return remote(block(b, core), block(b, core), up_send.at[s], up_recv.at[s], {"tp": other})

    def down_got(s):
        b = z + s
        return remote(block(b, core), block(b, core), down_send.at[s], down_recv.at[s], {"tp": other})

    locals_[2].wait()
    for o in range(1, n_dp):
        a2a[o - 1].wait_recv()

    for s in range(1, n_z + 1):
        if s > 1:
            @pl.when(z - s + 1 >= 0)
            def _():
                up_got(s - 1).wait_recv()

        if s < n_z:
            @pl.when((z - s + 1 >= 0) & (z + 1 < n_z))
            def _():
                up(s).start()

        if s > 1:
            @pl.when(z + s - 1 < n_z)
            def _():
                down_got(s - 1).wait_recv()

        if s < n_z:
            @pl.when((z + s - 1 < n_z) & (z - 1 >= 0))
            def _():
                down(s).start()

        if s == 1:
            to_pair(z).start()
        else:
            @pl.when(z - s + 1 >= 0)
            def _():
                to_pair(z - s + 1).start()

            @pl.when(z + s - 1 < n_z)
            def _():
                to_pair(z + s - 1).start()

        if s == 1:
            for copy in tp_copies:
                copy.wait_recv()
            gain_dp[dp, :, :] = jnp.sum(gain_tp[...], axis=0)
            for o in range(1, n_dp):
                copy = remote(gain_dp.at[dp], gain_dp.at[dp], gd_send.at[o], gd_recv.at[o], {"dp": dp_peer(o)})
                copy.start()
                sent.append(copy)
            for i in range(2, PIECES):
                send_own(i)
        if square and 2 <= s < 2 + half:
            forward(s - 2)
    if square:
        for i in range(max(n_z - 1, 0), half):
            forward(i)

    for b in range(n_z):
        remote(block(b, 1 - core), block(b, 1 - core), pair_send.at[b], pair_recv.at[b], {"tp": other}).wait_recv()

    width = min(256, sum_ref.shape[0])

    def multiply(origin, start, size, first=False):
        @pl.loop(0, sum_ref.shape[0] // width)
        def _(f):
            at = pl.ds(pl.multiple_of(f * width, width), width)
            part = lax.dot_general(
                xs[origin, pl.ds(start, size), at], kv[origin, pl.ds(start, size), :],
                (((0,), (0,)), ((), ())), preferred_element_type=jnp.float32,
            )
            if first:
                sum_ref[at, :] = part
            else:
                sum_ref[at, :] += part

    locals_[3].wait()
    multiply(dp, 0, tokens, True)
    for o in range(1, n_dp):
        if square and o == 3:
            continue
        for c in orders[o]:
            if not (square and c in orders[o][:half]):
                got(o, c)
        multiply(dp_peer(o), 0, tokens)

    for o in range(1, n_dp):
        remote(gain_dp.at[dp_peer(o)], gain_dp.at[dp_peer(o)], gd_send.at[o], gd_recv.at[o], {"dp": dp_peer(o)}).wait_recv()
    gain_ref[...] = jnp.sum(gain_dp[...], axis=0) / n_dp

    if square:
        for i in range(half):
            for o in (1, 2):
                c = orders[o][i]
                got(3, c)
                multiply(dp_peer(3), c * piece, piece)

    for copy in sent:
        copy.wait_send()
    for s in range(1, n_z):
        @pl.when((z - s + 1 >= 0) & (z + 1 < n_z))
        def _():
            up(s).wait_send()

        @pl.when((z + s - 1 < n_z) & (z - 1 >= 0))
        def _():
            down(s).wait_send()
    for b in range(n_z):
        to_pair(b).wait_send()


def square_kernel(
    n_tp, x_hbm, g_hbm, a_hbm, b_hbm, sum_ref, gain_ref,
    xs, xb, kv, kvp, part, arrived, a_buf, b_buf, gain_pair, gain_z, gain_dp,
    local_sem, head_send, head_recv, whole_send, whole_recv, fwd_send, fwd_recv,
    part_send, part_recv, a2a_send, a2a_recv,
    up_send, up_recv, down_send, down_recv, pair_send, pair_recv,
    gp_send, gp_recv, gz_send, gz_recv, gd_send, gd_recv,
):
    n_dp = 4
    dp = lax.axis_index("dp")
    tp = lax.axis_index("tp")
    z = tp // 2
    core = tp % 2
    n_z = n_tp // 2
    rows = g_hbm.shape[0]
    cols = kv.shape[2]
    tokens, features = x_hbm.shape
    head = part.shape[0]
    tail = features - head
    chunk = head // HEADS
    half = tokens // 2
    other = 2 * z + 1 - core
    sent = []

    def dp_peer(o):
        return jnp.bitwise_xor(dp, o)

    def remote(src, dst, send, recv, where):
        return pltpu.make_async_remote_copy(
            src_ref=src, dst_ref=dst, send_sem=send, recv_sem=recv,
            device_id=where, device_id_type=pl.DeviceIdType.MESH,
        )

    def go(copy):
        copy.start()
        sent.append(copy)

    my_rows = pl.ds(pl.multiple_of(tp * rows, rows), rows)

    def g_cols(d):
        return g_hbm.at[:, pl.ds(pl.multiple_of(d * cols, cols), cols)]

    locals_ = [
        pltpu.make_async_copy(g_cols(dp_peer(2)), kvp.at[0, my_rows, :], local_sem.at[0]),
        pltpu.make_async_copy(a_hbm, a_buf, local_sem.at[1]),
        pltpu.make_async_copy(b_hbm, b_buf, local_sem.at[2]),
        pltpu.make_async_copy(g_cols(dp), kv.at[dp, my_rows, :], local_sem.at[3]),
        pltpu.make_async_copy(x_hbm, xs.at[0], local_sem.at[4]),
    ]
    for copy in locals_:
        copy.start()

    barrier = pltpu.get_barrier_semaphore()
    for o in range(1, n_dp):
        pl.semaphore_signal(barrier, inc=1, device_id={"dp": dp_peer(o)}, device_id_type=pl.DeviceIdType.MESH)
    for o in range(1, n_tp):
        pl.semaphore_signal(barrier, inc=1, device_id={"tp": lax.rem(tp + o, n_tp)}, device_id_type=pl.DeviceIdType.MESH)
    pl.semaphore_wait(barrier, n_dp - 1 + n_tp - 1)

    pair_base = dp // 2 * 2
    groups = [
        kvp.at[pl.ds(0, 1)],
        kvp.at[pl.ds(1, 1)],
        kv.at[pl.ds(pair_base, 2)],
        kv.at[pl.ds(2 - pair_base, 2)],
    ]

    def block(g, b, c):
        return groups[g].at[:, pl.ds(pl.multiple_of((2 * b + c) * rows, rows), rows), :]

    def to_pair(g, b):
        return remote(block(g, b, core), block(g, b, core), pair_send.at[g, b], pair_recv.at[g, b], {"tp": other})

    def from_pair(g, b):
        return remote(block(g, b, 1 - core), block(g, b, 1 - core), pair_send.at[g, b], pair_recv.at[g, b], {"tp": other})

    def up(g, s):
        b = z - s + 1
        return remote(block(g, b, core), block(g, b, core), up_send.at[g, s], up_recv.at[g, s], {"tp": tp + 2})

    def down(g, s):
        b = z + s - 1
        return remote(block(g, b, core), block(g, b, core), down_send.at[g, s], down_recv.at[g, s], {"tp": tp - 2})

    def up_got(g, s):
        b = z - s
        return remote(block(g, b, core), block(g, b, core), up_send.at[g, s], up_recv.at[g, s], {"tp": other})

    def down_got(g, s):
        b = z + s
        return remote(block(g, b, core), block(g, b, core), down_send.at[g, s], down_recv.at[g, s], {"tp": other})

    def chain(g, s):
        if s > 1:
            @pl.when(z - s + 1 >= 0)
            def _():
                up_got(g, s - 1).wait_recv()

        if s < n_z:
            @pl.when((z - s + 1 >= 0) & (z + 1 < n_z))
            def _():
                up(g, s).start()

        if s > 1:
            @pl.when(z + s - 1 < n_z)
            def _():
                down_got(g, s - 1).wait_recv()

        if s < n_z:
            @pl.when((z + s - 1 < n_z) & (z - 1 >= 0))
            def _():
                down(g, s).start()

        if s == 1:
            to_pair(g, z).start()
        else:
            @pl.when(z - s + 1 >= 0)
            def _():
                to_pair(g, z - s + 1).start()

            @pl.when(z + s - 1 < n_z)
            def _():
                to_pair(g, z + s - 1).start()

    def complete(g):
        for b in range(n_z):
            from_pair(g, b).wait_recv()

    swap = remote(g_cols(dp_peer(3)), kvp.at[1, my_rows, :], a2a_send.at[0], a2a_recv.at[0], {"dp": dp_peer(1)})
    go(swap)
    locals_[0].wait()
    chain(0, 1)

    def a2a(o, origin):
        return remote(g_cols(dp_peer(o)), kv.at[origin, my_rows, :], a2a_send.at[o], a2a_recv.at[o], {"dp": dp_peer(o)})

    for o in range(1, n_dp):
        go(a2a(o, dp))

    tail_at = pl.ds(head, tail)

    def head_copy(k):
        at = pl.ds(k * chunk, chunk)
        return remote(x_hbm.at[:, at], xs.at[1, :, at], head_send.at[k], head_recv.at[k], {"dp": dp_peer(1)})

    def tail_copy(o, h):
        at = pl.ds(h * half, half)
        dst = xs.at[1, at, tail_at] if o == 1 else xb.at[0, at, :]
        return remote(x_hbm.at[at, tail_at], dst, whole_send.at[o, h], whole_recv.at[o, h], {"dp": dp_peer(o)})

    def forward(h):
        at = pl.ds(h * half, half)
        src = xs.at[1, at, tail_at] if h == 0 else xb.at[0, at, :]
        return remote(src, xb.at[1, at, :], fwd_send.at[h], fwd_recv.at[h], {"dp": dp_peer(2 - h)})

    early = HEADS // 2
    for k in range(early):
        go(head_copy(k))
    go(tail_copy(2, 1))
    go(tail_copy(2, 0))

    locals_[1].wait()
    locals_[2].wait()
    wide = gain_pair.shape[2]

    def gain_lines(lo, hi):
        for j in range(lo, hi):
            at = pl.ds(j * wide, wide)
            products = a_buf[:, at].astype(jnp.float32) * b_buf[:, at].astype(jnp.float32)
            gain_pair[core, pl.ds(j, 1), :] = jnp.sum(products, axis=0, keepdims=True)

    lines = gain_pair.shape[1]
    gain_lines(0, lines)
    swap.wait_recv()
    chain(1, 1)
    gain_core = remote(gain_pair.at[core], gain_pair.at[core], gp_send.at[0], gp_recv.at[0], {"tp": other})
    go(gain_core)
    for s in range(2, n_z + 1):
        chain(0, s)
        chain(1, s)

    gain_core.wait_recv()
    gain_z[z, :, :] = jnp.sum(gain_pair[...], axis=0)
    for o in range(1, n_z):
        go(remote(gain_z.at[z], gain_z.at[z], gz_send.at[o], gz_recv.at[o], {"tp": lax.rem(tp + 2 * o, n_tp)}))

    for o in (1, 2, 3):
        a2a(o, dp_peer(o)).wait_recv()
    locals_[3].wait()
    chain(2, 1)
    locals_[4].wait()
    for k in range(early, HEADS):
        go(head_copy(k))
    complete(0)
    complete(1)

    def dot(x, w):
        return lax.dot_general(x, w, (((0,), (0,)), ((), ())), preferred_element_type=jnp.float32)

    def part_copy(k):
        at = pl.ds(k * chunk, chunk)
        return remote(part.at[at, :], arrived.at[at, :], part_send.at[k], part_recv.at[k], {"dp": dp_peer(2)})

    for k in range(HEADS):
        at = pl.ds(k * chunk, chunk)
        head_copy(k).wait_recv()
        part[at, :] = dot(xs[0, :, at], kvp[0]) + dot(xs[1, :, at], kvp[1])
        go(part_copy(k))
        if k == 1:
            for o in range(1, n_z):
                copy = remote(
                    gain_z.at[lax.rem(z + o, n_z)], gain_z.at[lax.rem(z + o, n_z)],
                    gz_send.at[n_z - o], gz_recv.at[n_z - o], {"tp": other},
                )
                copy.wait_recv()
            gain_dp[dp, :, :] = jnp.sum(gain_z[...], axis=0)
            for o in range(1, n_dp):
                go(remote(gain_dp.at[dp], gain_dp.at[dp], gd_send.at[o], gd_recv.at[o], {"dp": dp_peer(o)}))
            chain(2, 2)
        if k == 2:
            go(tail_copy(1, 0))
            go(tail_copy(1, 1))
        if k == 3:
            tail_copy(2, 1).wait_recv()
            go(forward(1))
            chain(2, 3)
            chain(3, 1)
        if k == HEADS - 2:
            for s in range(4, n_z + 1):
                chain(2, s)
    complete(2)
    chain(3, 2)

    def head_sum(k):
        at = pl.ds(k * chunk, chunk)
        sum_ref[at, :] = dot(xs[0, :, at], kv[dp]) + dot(xs[1, :, at], kv[dp_peer(1)])

    for k in range(HEADS // 2):
        head_sum(k)
    tail_copy(1, 0).wait_recv()
    go(forward(0))
    chain(3, 3)
    for k in range(HEADS // 2, HEADS):
        head_sum(k)
    tail_copy(1, 1).wait_recv()
    sum_ref[tail_at, :] = dot(xs[0, :, tail_at], kv[dp]) + dot(xs[1, :, tail_at], kv[dp_peer(1)])
    for s in range(4, n_z + 1):
        chain(3, s)
    for o in range(1, n_dp):
        remote(gain_dp.at[dp_peer(o)], gain_dp.at[dp_peer(o)], gd_send.at[o], gd_recv.at[o], {"dp": dp_peer(o)}).wait_recv()
    total_gain = jnp.sum(gain_dp[...], axis=0) / n_dp
    for i in range(wide // 128):
        gain_ref[pl.ds(i, lines, stride=wide // 128), :] = total_gain[:, i * 128:(i + 1) * 128]
    for k in range(HEADS):
        at = pl.ds(k * chunk, chunk)
        part_copy(k).wait_recv()
        sum_ref[at, :] += arrived[at, :]
    complete(3)
    tail_copy(2, 0).wait_recv()
    sum_ref[tail_at, :] += dot(xb[0], kv[dp_peer(2)])
    for h in (1, 0):
        forward(h).wait_recv()
        at = pl.ds(h * half, half)
        sum_ref[tail_at, :] += dot(xb[1, at, :], kv[dp_peer(3), at, :])

    for copy in sent:
        copy.wait_send()
    for g in range(len(groups)):
        for s in range(1, n_z):
            @pl.when((z - s + 1 >= 0) & (z + 1 < n_z))
            def _():
                up(g, s).wait_send()

            @pl.when((z + s - 1 < n_z) & (z - 1 >= 0))
            def _():
                down(g, s).wait_send()
        for b in range(n_z):
            to_pair(g, b).wait_send()


def square_call(layer, n_tp, x, g, a, b):
    tokens, features = x.shape
    rows, width = g.shape
    model = a.shape[1]
    n_dp = 4
    cols = width // n_dp
    lines = 8
    n_z = n_tp // 2
    head = features // (HEADS + 2) * HEADS
    dma = pltpu.SemaphoreType.DMA
    bf16, f32 = jnp.bfloat16, jnp.float32
    buffers = [
        ((2, tokens, features), bf16), ((2, tokens, features - head), bf16),
        ((n_dp, tokens, cols), bf16), ((2, tokens, cols), bf16),
        ((head, cols), f32), ((head, cols), f32),
        ((rows, model), bf16), ((rows, model), bf16),
        ((2, lines, model // lines), f32), ((n_z, lines, model // lines), f32), ((n_dp, lines, model // lines), f32),
    ]
    return pl.pallas_call(
        functools.partial(square_kernel, n_tp),
        out_shape=(
            jax.ShapeDtypeStruct((features, cols), f32),
            jax.ShapeDtypeStruct((model // 128, 128), f32),
        ),
        in_specs=[pl.BlockSpec(memory_space=pltpu.HBM)] * 4,
        out_specs=(pl.BlockSpec(memory_space=pltpu.VMEM), pl.BlockSpec(memory_space=pltpu.VMEM)),
        scratch_shapes=[pltpu.VMEM(shape, dtype) for shape, dtype in buffers] + [
            dma((5,)), dma((HEADS,)), dma((HEADS,)), dma((3, 2)), dma((3, 2)), dma((2,)), dma((2,)),
            dma((HEADS,)), dma((HEADS,)), dma((n_dp,)), dma((n_dp,)),
        ] + [dma((4, n_z))] * 6 + [
            dma((1,)), dma((1,)), dma((n_z,)), dma((n_z,)), dma((n_dp,)), dma((n_dp,)),
        ],
        compiler_params=pltpu.CompilerParams(
            collective_id=layer, has_side_effects=True, vmem_limit_bytes=50 * 1024 * 1024,
        ),
    )(x, g, a, b)


def shards(n_dp, n_tp, proj_in, kv_grad, normed, norm_grad, first_moment, second_moment):
    layers, tokens, features = proj_in.shape
    rows, width = kv_grad.shape[1:]
    model = normed.shape[2]
    cols = width // n_dp
    lines = 8
    dma = pltpu.SemaphoreType.DMA
    n_z = n_tp // 2
    firsts, seconds, updates, gains = [], [], [], []
    for layer in range(layers):
        if n_dp == 4 and features % (128 * (HEADS + 2)) == 0 and n_tp >= 6:
            total, gain = square_call(layer, n_tp, proj_in[layer], kv_grad[layer], normed[layer], norm_grad[layer])
        else:
            total, gain = pl.pallas_call(
                functools.partial(kernel, n_dp, n_tp),
                out_shape=(
                    jax.ShapeDtypeStruct((features, cols), jnp.float32),
                    jax.ShapeDtypeStruct((lines, model // lines), jnp.float32),
                ),
                in_specs=[pl.BlockSpec(memory_space=pltpu.HBM)] * 4,
                out_specs=(pl.BlockSpec(memory_space=pltpu.VMEM), pl.BlockSpec(memory_space=pltpu.VMEM)),
                scratch_shapes=[
                    pltpu.VMEM((n_dp, tokens, features), jnp.bfloat16),
                    pltpu.VMEM((n_dp, n_tp * rows, cols), jnp.bfloat16),
                    pltpu.VMEM((rows, model), jnp.bfloat16),
                    pltpu.VMEM((rows, model), jnp.bfloat16),
                    pltpu.VMEM((n_tp, lines, model // lines), jnp.float32),
                    pltpu.VMEM((n_dp, lines, model // lines), jnp.float32),
                    dma((4,)),
                    dma((n_dp, PIECES)), dma((n_dp, PIECES)),
                    dma((n_dp,)), dma((n_dp,)),
                    dma((n_z,)), dma((n_z,)), dma((n_z,)), dma((n_z,)),
                    dma((n_z,)), dma((n_z,)),
                    dma((n_tp,)), dma((n_tp,)), dma((n_dp,)), dma((n_dp,)),
                ],
                compiler_params=pltpu.CompilerParams(
                    collective_id=layer, has_side_effects=True, vmem_limit_bytes=60 * 1024 * 1024,
                ),
            )(proj_in[layer], kv_grad[layer], normed[layer], norm_grad[layer])
        new_first, new_second, update = adam_update(total / n_dp, first_moment[layer], second_moment[layer])
        firsts.append(new_first)
        seconds.append(new_second)
        updates.append(update)
        gains.append(gain.reshape(model))
    return (jnp.stack(firsts), jnp.stack(seconds), jnp.stack(updates), jnp.stack(gains))


def solution(mesh):
    return jax.shard_map(
        functools.partial(shards, mesh.shape["dp"], mesh.shape["tp"]),
        mesh=mesh,
        in_specs=(
            P(None, "dp", "tp"),
            P(None, ("dp", "tp"), None),
            P(None, ("dp", "tp"), None),
            P(None, ("dp", "tp"), None),
            P(None, "tp", "dp"),
            P(None, "tp", "dp"),
        ),
        out_specs=(P(None, "tp", "dp"), P(None, "tp", "dp"), P(None, "tp", "dp"), P()),
        check_vma=False,
    )
```

profile of v0, /device:TPU:0, one launch (start us, length us, event | category | flops | bytes accessed | tf_op | source)
XLA Modules:
  0.0 79.8 jit_solution(6663524581731930500)
XLA Ops:
  0.6 0.0 copy-start
  0.6 1.0 %copy-done = bf16[1,128,2048]{2,1,0:T(8,128)(2,1)S(1)} copy-done((bf16[1,128,2048]{2,1,0:T(8,128)(2,1)S(1)}, bf16[1,128,2048]{2,1,0:T(8,128)(2,1)}, u32[]{:S(2)}) %copy-start) | copy-done | bytes 524312
  1.7 0.0 copy-start.1
  1.7 0.0 copy-start.2
  1.7 73.8 %shard_map.93 = (f32[1024,512]{1,0:T(8,128)S(1)}, f32[64,128]{1,0:T(8,128)S(1)}) custom-call(bf16[1024,1024]{1,0:T(8,128)(2,1)} %bitcast.25, bf16[128,2048]{1,0:T(8,128)(2,1)S(1)} %bitcast.23, bf16[128,8192]{1,0:T(8,128)(2,1)} %bitcast.26, bf16[128,8192]{1,0:T(8,128)(2,1)} %bitcast.27), custom_call_target="tpu_custom_call" | custom-call | tf_op jit(solution)/shard_map/pallas_call | solution.py:567
  75.5 0.0 copy-done.1
  75.5 0.0 copy-done.2
  75.6 3.6 %divide_bitcast_fusion = (f32[1,1024,512]{2,1,0:T(8,128)}, f32[1,1024,512]{2,1,0:T(8,128)}, f32[1,1024,512]{2,1,0:T(8,128)}) fusion(f32[1024,512]{1,0:T(8,128)S(1)} %get-tuple-element.6, f32[1,1024,512]{2,1,0:T(8,128)S(1)} %copy-done.1, f32[1,1024,512]{2,1,0:T(8,128)S(1)} %copy-done.2), kind=kLoop, calls=%fused_computation.2 | loop fusion | flops 6291456 | bytes 12582912 | tf_op jit(solution)/shard_map/stack | solution.py:631
  79.1 0.6 copy.11
Async XLA Ops:
  0.6 1.0 %copy-start = (bf16[1,128,2048]{2,1,0:T(8,128)(2,1)S(1)}, bf16[1,128,2048]{2,1,0:T(8,128)(2,1)}, u32[]{:S(2)}) copy-start(bf16[1,128,2048]{2,1,0:T(8,128)(2,1)} %param.7) | copy-start | bytes 1572868
  1.7 73.9 %copy-start.1 = (f32[1,1024,512]{2,1,0:T(8,128)S(1)}, f32[1,1024,512]{2,1,0:T(8,128)}, u32[]{:S(2)}) copy-start(f32[1,1024,512]{2,1,0:T(8,128)} %param.10) | copy-start | bytes 6291460
  1.7 73.9 %copy-start.2 = (f32[1,1024,512]{2,1,0:T(8,128)S(1)}, f32[1,1024,512]{2,1,0:T(8,128)}, u32[]{:S(2)}) copy-start(f32[1,1024,512]{2,1,0:T(8,128)} %param.11) | copy-start | bytes 6291460
where the time goes:
time: 79.9 us; the launch traced here: 79.8 us
  Pallas kernels  73.8 us (92%)
  other arithmetic  3.59 us (4%)
  local copies, waits for them, and re-layouts  1.66 us (2%)
    pallas_call x1, Pallas kernels, square_call(): pl.pallas_call(functools.partial(square_kernel, n_tp), out_shape=(jax.Sha...  73.8 us
    another operation x1, other arithmetic, shards(): jnp.stack(updates)  3.59 us
    unnamed x7, local copies, waits for them, and re-layouts  1.66 us

commit v1 on v0

--- a/solution.py
+++ b/solution.py
@@ -1,4 +1,5 @@
 import functools
+import math
 
 import jax
 import jax.numpy as jnp
@@ -13,7 +14,10 @@
 correct_two = 0.0975
 epsilon = 1e-08
 PIECES = 4
-HEADS = 6
+LANES = 128
+SPAN = 250.0
+KNEE = 2.0 ** -5
+VMEM_LIMIT = 46 * 1024 * 1024
 
 
 def adam_update(mean_grad, first_old, second_old):
@@ -266,13 +270,24 @@
         to_pair(b).wait_send()
 
 
-def square_kernel(
-    n_tp, x_hbm, g_hbm, a_hbm, b_hbm, sum_ref, gain_ref,
-    xs, xb, kv, kvp, part, arrived, a_buf, b_buf, gain_pair, gain_z, gain_dp,
-    local_sem, head_send, head_recv, whole_send, whole_recv, fwd_send, fwd_recv,
-    part_send, part_recv, a2a_send, a2a_recv,
-    up_send, up_recv, down_send, down_recv, pair_send, pair_recv,
-    gp_send, gp_recv, gz_send, gz_recv, gd_send, gd_recv,
+def encode(value, bound):
+    power = SPAN / math.log2(1.0 + bound / KNEE)
+    code = jnp.exp2(power * jnp.log2(1.0 + jnp.abs(value) * (1.0 / KNEE)) - SPAN / 2)
+    return jnp.where(value < 0.0, -code, code).astype(jnp.bfloat16)
+
+
+def decode(code, bound):
+    power = SPAN / math.log2(1.0 + bound / KNEE)
+    code = code.astype(jnp.float32)
+    value = (jnp.exp2((jnp.log2(jnp.abs(code)) + SPAN / 2) * (1.0 / power)) - 1.0) * KNEE
+    return jnp.where(code < 0.0, -value, value)
+
+
+def pair_kernel(
+    n_tp, x_hbm, g_hbm, a_hbm, b_hbm, m_hbm, v_hbm, first_ref, second_ref, step_ref, gain_ref,
+    xs, kv, part, arrived, own, m_buf, v_buf, a_buf, b_buf, gain_half, gain_pair, gain_x, gain_y, gain_z, gain_all,
+    local_sem, swap_send, swap_recv, x_send, x_recv, part_send, part_recv,
+    up_send, up_recv, down_send, down_recv, pair_send, pair_recv, gain_send, gain_recv,
 ):
     n_dp = 4
     dp = lax.axis_index("dp")
@@ -283,15 +298,12 @@
     rows = g_hbm.shape[0]
     cols = kv.shape[2]
     tokens, features = x_hbm.shape
-    head = part.shape[0]
-    tail = features - head
-    chunk = head // HEADS
-    half = tokens // 2
+    chunks = features // LANES
+    bound = 2.0 * tokens * 6.0 * 0.75
     other = 2 * z + 1 - core
+    beside = jnp.bitwise_xor(dp, 1)
+    across = jnp.bitwise_xor(dp, 2)
     sent = []
-
-    def dp_peer(o):
-        return jnp.bitwise_xor(dp, o)
 
     def remote(src, dst, send, recv, where):
         return pltpu.make_async_remote_copy(
@@ -309,32 +321,56 @@
         return g_hbm.at[:, pl.ds(pl.multiple_of(d * cols, cols), cols)]
 
     locals_ = [
-        pltpu.make_async_copy(g_cols(dp_peer(2)), kvp.at[0, my_rows, :], local_sem.at[0]),
-        pltpu.make_async_copy(a_hbm, a_buf, local_sem.at[1]),
-        pltpu.make_async_copy(b_hbm, b_buf, local_sem.at[2]),
-        pltpu.make_async_copy(g_cols(dp), kv.at[dp, my_rows, :], local_sem.at[3]),
+        pltpu.make_async_copy(g_cols(across), kv.at[0, my_rows, :], local_sem.at[0]),
+        pltpu.make_async_copy(g_cols(dp), kv.at[2, my_rows, :], local_sem.at[1]),
+        pltpu.make_async_copy(a_hbm, a_buf, local_sem.at[2]),
+        pltpu.make_async_copy(b_hbm, b_buf, local_sem.at[3]),
         pltpu.make_async_copy(x_hbm, xs.at[0], local_sem.at[4]),
+        pltpu.make_async_copy(m_hbm, m_buf, local_sem.at[5]),
+        pltpu.make_async_copy(v_hbm, v_buf, local_sem.at[6]),
     ]
     for copy in locals_:
         copy.start()
 
     barrier = pltpu.get_barrier_semaphore()
-    for o in range(1, n_dp):
-        pl.semaphore_signal(barrier, inc=1, device_id={"dp": dp_peer(o)}, device_id_type=pl.DeviceIdType.MESH)
-    for o in range(1, n_tp):
-        pl.semaphore_signal(barrier, inc=1, device_id={"tp": lax.rem(tp + o, n_tp)}, device_id_type=pl.DeviceIdType.MESH)
-    pl.semaphore_wait(barrier, n_dp - 1 + n_tp - 1)
-
-    pair_base = dp // 2 * 2
-    groups = [
-        kvp.at[pl.ds(0, 1)],
-        kvp.at[pl.ds(1, 1)],
-        kv.at[pl.ds(pair_base, 2)],
-        kv.at[pl.ds(2 - pair_base, 2)],
-    ]
+
+    def hello(where):
+        pl.semaphore_signal(barrier, inc=1, device_id=where, device_id_type=pl.DeviceIdType.MESH)
+
+    hello({"dp": beside})
+    hello({"dp": across})
+    hello({"tp": other})
+
+    @pl.when(z + 1 < n_z)
+    def _():
+        hello({"tp": tp + 2})
+
+    @pl.when(z >= 1)
+    def _():
+        hello({"tp": tp - 2})
+
+    pl.semaphore_wait(barrier, 3 + jnp.where(z + 1 < n_z, 1, 0) + jnp.where(z >= 1, 1, 0))
+
+    def swap(i, plane, d):
+        return remote(g_cols(d), kv.at[plane, my_rows, :], swap_send.at[i], swap_recv.at[i], {"dp": beside})
+
+    swaps = [swap(0, 1, jnp.bitwise_xor(dp, 3)), swap(1, 3, beside)]
+
+    def x_copy(k):
+        at = pl.ds(k * LANES, LANES)
+        return remote(x_hbm.at[:, at], xs.at[1, :, at], x_send.at[k], x_recv.at[k], {"dp": beside})
+
+    go(swaps[0])
+    go(swaps[1])
+    for k in range(chunks):
+        go(x_copy(k))
+
+    GAIN = 4
 
     def block(g, b, c):
-        return groups[g].at[:, pl.ds(pl.multiple_of((2 * b + c) * rows, rows), rows), :]
+        if g == GAIN:
+            return gain_z.at[b]
+        return kv.at[g, pl.ds(pl.multiple_of((2 * b + c) * rows, rows), rows), :]
 
     def to_pair(g, b):
         return remote(block(g, b, core), block(g, b, core), pair_send.at[g, b], pair_recv.at[g, b], {"tp": other})
@@ -379,6 +415,8 @@
             def _():
                 down(g, s).start()
 
+        if g == GAIN:
+            return
         if s == 1:
             to_pair(g, z).start()
         else:
@@ -394,146 +432,130 @@
         for b in range(n_z):
             from_pair(g, b).wait_recv()
 
-    swap = remote(g_cols(dp_peer(3)), kvp.at[1, my_rows, :], a2a_send.at[0], a2a_recv.at[0], {"dp": dp_peer(1)})
-    go(swap)
+    def gain_copy(i, src, dst, where):
+        return remote(src, dst, gain_send.at[i], gain_recv.at[i], where)
+
+    def dot(x, w):
+        return lax.dot_general(x, w, (((0,), (0,)), ((), ())), preferred_element_type=jnp.float32)
+
+    halves = 2
+    wide = cols // halves
+
+    def part_copy(k, h):
+        at = (pl.ds(k * LANES, LANES), pl.ds(h * wide, wide))
+        return remote(part.at[at], arrived.at[at], part_send.at[k, h], part_recv.at[k, h], {"dp": across})
+
+    def partial(k):
+        at = pl.ds(k * LANES, LANES)
+        x_copy(k).wait_recv()
+        for h in range(halves):
+            ch = pl.ds(h * wide, wide)
+            total = dot(xs[0, :, at], kv[0, :, ch]) + dot(xs[1, :, at], kv[1, :, ch])
+            part[at, ch] = encode(total, bound)
+            go(part_copy(k, h))
+
+    def own_sum(k):
+        at = pl.ds(k * LANES, LANES)
+        own[at, :] = dot(xs[0, :, at], kv[2]) + dot(xs[1, :, at], kv[3])
+
+    def finish(k):
+        at = pl.ds(k * LANES, LANES)
+        for h in range(halves):
+            ch = pl.ds(h * wide, wide)
+            part_copy(k, h).wait_recv()
+            mean = (own[at, ch] + decode(arrived[at, ch], bound)) / n_dp
+            new_first, new_second, update = adam_update(mean, m_buf[at, ch], v_buf[at, ch])
+            first_ref[at, ch] = new_first
+            second_ref[at, ch] = new_second
+            step_ref[at, ch] = update
+
     locals_[0].wait()
     chain(0, 1)
-
-    def a2a(o, origin):
-        return remote(g_cols(dp_peer(o)), kv.at[origin, my_rows, :], a2a_send.at[o], a2a_recv.at[o], {"dp": dp_peer(o)})
-
-    for o in range(1, n_dp):
-        go(a2a(o, dp))
-
-    tail_at = pl.ds(head, tail)
-
-    def head_copy(k):
-        at = pl.ds(k * chunk, chunk)
-        return remote(x_hbm.at[:, at], xs.at[1, :, at], head_send.at[k], head_recv.at[k], {"dp": dp_peer(1)})
-
-    def tail_copy(o, h):
-        at = pl.ds(h * half, half)
-        dst = xs.at[1, at, tail_at] if o == 1 else xb.at[0, at, :]
-        return remote(x_hbm.at[at, tail_at], dst, whole_send.at[o, h], whole_recv.at[o, h], {"dp": dp_peer(o)})
-
-    def forward(h):
-        at = pl.ds(h * half, half)
-        src = xs.at[1, at, tail_at] if h == 0 else xb.at[0, at, :]
-        return remote(src, xb.at[1, at, :], fwd_send.at[h], fwd_recv.at[h], {"dp": dp_peer(2 - h)})
-
-    early = HEADS // 2
-    for k in range(early):
-        go(head_copy(k))
-    go(tail_copy(2, 1))
-    go(tail_copy(2, 0))
-
     locals_[1].wait()
+    chain(2, 1)
+
     locals_[2].wait()
-    wide = gain_pair.shape[2]
-
-    def gain_lines(lo, hi):
-        for j in range(lo, hi):
-            at = pl.ds(j * wide, wide)
+    locals_[3].wait()
+    lines, span = gain_half.shape[1:]
+    for h in range(2):
+        for j in range(lines):
+            at = pl.ds((h * lines + j) * span, span)
             products = a_buf[:, at].astype(jnp.float32) * b_buf[:, at].astype(jnp.float32)
-            gain_pair[core, pl.ds(j, 1), :] = jnp.sum(products, axis=0, keepdims=True)
-
-    lines = gain_pair.shape[1]
-    gain_lines(0, lines)
-    swap.wait_recv()
+            gain_half[h, pl.ds(j, 1), :] = jnp.sum(products, axis=0, keepdims=True)
+    go(gain_copy(0, gain_half.at[1 - core], gain_pair.at[1], {"tp": other}))
+    swaps[0].wait_recv()
     chain(1, 1)
-    gain_core = remote(gain_pair.at[core], gain_pair.at[core], gp_send.at[0], gp_recv.at[0], {"tp": other})
-    go(gain_core)
-    for s in range(2, n_z + 1):
+    chain(0, 2)
+    gain_copy(0, gain_half.at[1 - core], gain_pair.at[1], {"tp": other}).wait_recv()
+    gain_x[0] = gain_half[core] + gain_pair[1]
+    go(gain_copy(1, gain_x.at[0], gain_x.at[1], {"dp": beside}))
+    chain(1, 2)
+    chain(0, 3)
+    chain(1, 3)
+    swaps[1].wait_recv()
+    chain(3, 1)
+    chain(2, 2)
+    for s in range(4, n_z + 1):
         chain(0, s)
         chain(1, s)
-
-    gain_core.wait_recv()
-    gain_z[z, :, :] = jnp.sum(gain_pair[...], axis=0)
-    for o in range(1, n_z):
-        go(remote(gain_z.at[z], gain_z.at[z], gz_send.at[o], gz_recv.at[o], {"tp": lax.rem(tp + 2 * o, n_tp)}))
-
-    for o in (1, 2, 3):
-        a2a(o, dp_peer(o)).wait_recv()
-    locals_[3].wait()
-    chain(2, 1)
-    locals_[4].wait()
-    for k in range(early, HEADS):
-        go(head_copy(k))
     complete(0)
     complete(1)
-
-    def dot(x, w):
-        return lax.dot_general(x, w, (((0,), (0,)), ((), ())), preferred_element_type=jnp.float32)
-
-    def part_copy(k):
-        at = pl.ds(k * chunk, chunk)
-        return remote(part.at[at, :], arrived.at[at, :], part_send.at[k], part_recv.at[k], {"dp": dp_peer(2)})
-
-    for k in range(HEADS):
-        at = pl.ds(k * chunk, chunk)
-        head_copy(k).wait_recv()
-        part[at, :] = dot(xs[0, :, at], kvp[0]) + dot(xs[1, :, at], kvp[1])
-        go(part_copy(k))
-        if k == 1:
-            for o in range(1, n_z):
-                copy = remote(
-                    gain_z.at[lax.rem(z + o, n_z)], gain_z.at[lax.rem(z + o, n_z)],
-                    gz_send.at[n_z - o], gz_recv.at[n_z - o], {"tp": other},
-                )
-                copy.wait_recv()
-            gain_dp[dp, :, :] = jnp.sum(gain_z[...], axis=0)
-            for o in range(1, n_dp):
-                go(remote(gain_dp.at[dp], gain_dp.at[dp], gd_send.at[o], gd_recv.at[o], {"dp": dp_peer(o)}))
-            chain(2, 2)
-        if k == 2:
-            go(tail_copy(1, 0))
-            go(tail_copy(1, 1))
-        if k == 3:
-            tail_copy(2, 1).wait_recv()
-            go(forward(1))
-            chain(2, 3)
-            chain(3, 1)
-        if k == HEADS - 2:
-            for s in range(4, n_z + 1):
-                chain(2, s)
+    locals_[4].wait()
+
+    partial(0)
+    gain_copy(1, gain_x.at[0], gain_x.at[1], {"dp": beside}).wait_recv()
+    gain_y[0] = gain_x[0] + gain_x[1]
+    go(gain_copy(2, gain_y.at[0], gain_y.at[1], {"dp": across}))
+    chain(3, 2)
+    chain(2, 3)
+    partial(1)
+    gain_copy(2, gain_y.at[0], gain_y.at[1], {"dp": across}).wait_recv()
+    gain_z[z] = gain_y[0] + gain_y[1]
+    chain(GAIN, 1)
+    chain(3, 3)
+    partial(2)
+    chain(GAIN, 2)
+    for s in range(4, n_z + 1):
+        chain(2, s)
+        chain(3, s)
+    partial(3)
+    for s in range(3, n_z + 1):
+        chain(GAIN, s)
     complete(2)
-    chain(3, 2)
-
-    def head_sum(k):
-        at = pl.ds(k * chunk, chunk)
-        sum_ref[at, :] = dot(xs[0, :, at], kv[dp]) + dot(xs[1, :, at], kv[dp_peer(1)])
-
-    for k in range(HEADS // 2):
-        head_sum(k)
-    tail_copy(1, 0).wait_recv()
-    go(forward(0))
-    chain(3, 3)
-    for k in range(HEADS // 2, HEADS):
-        head_sum(k)
-    tail_copy(1, 1).wait_recv()
-    sum_ref[tail_at, :] = dot(xs[0, :, tail_at], kv[dp]) + dot(xs[1, :, tail_at], kv[dp_peer(1)])
-    for s in range(4, n_z + 1):
-        chain(3, s)
-    for o in range(1, n_dp):
-        remote(gain_dp.at[dp_peer(o)], gain_dp.at[dp_peer(o)], gd_send.at[o], gd_recv.at[o], {"dp": dp_peer(o)}).wait_recv()
-    total_gain = jnp.sum(gain_dp[...], axis=0) / n_dp
-    for i in range(wide // 128):
-        gain_ref[pl.ds(i, lines, stride=wide // 128), :] = total_gain[:, i * 128:(i + 1) * 128]
-    for k in range(HEADS):
-        at = pl.ds(k * chunk, chunk)
-        part_copy(k).wait_recv()
-        sum_ref[at, :] += arrived[at, :]
     complete(3)
-    tail_copy(2, 0).wait_recv()
-    sum_ref[tail_at, :] += dot(xb[0], kv[dp_peer(2)])
-    for h in (1, 0):
-        forward(h).wait_recv()
-        at = pl.ds(h * half, half)
-        sum_ref[tail_at, :] += dot(xb[1, at, :], kv[dp_peer(3), at, :])
+    own_sum(0)
+    own_sum(1)
+    gain_all[core] = jnp.sum(gain_z[...], axis=0) / n_dp
+    go(gain_copy(3, gain_all.at[core], gain_all.at[core], {"tp": other}))
+    for copy in locals_[5:]:
+        copy.wait()
+    finish(0)
+    done, finished = 2, 1
+    for k in range(4, chunks):
+        partial(k)
+        while done < k:
+            own_sum(done)
+            done += 1
+            if finished < done - 1:
+                finish(finished)
+                finished += 1
+        if k == 4:
+            gain_copy(3, gain_all.at[1 - core], gain_all.at[1 - core], {"tp": other}).wait_recv()
+            per = span // LANES
+            for h in range(2):
+                for i in range(per):
+                    at = pl.ds(h * lines * per + i, lines, stride=per)
+                    gain_ref[at, :] = gain_all[h, :, i * LANES:(i + 1) * LANES]
+    while done < chunks:
+        own_sum(done)
+        done += 1
+    while finished < chunks:
+        finish(finished)
+        finished += 1
 
     for copy in sent:
         copy.wait_send()
-    for g in range(len(groups)):
+    for g in range(GAIN + 1):
         for s in range(1, n_z):
             @pl.when((z - s + 1 >= 0) & (z + 1 < n_z))
             def _():
@@ -542,46 +564,63 @@
             @pl.when((z + s - 1 < n_z) & (z - 1 >= 0))
             def _():
                 down(g, s).wait_send()
-        for b in range(n_z):
-            to_pair(g, b).wait_send()
-
-
-def square_call(layer, n_tp, x, g, a, b):
+        if g < GAIN:
+            for b in range(n_z):
+                to_pair(g, b).wait_send()
+
+
+def store_kernel(*refs):
+    count = (len(refs) - 1) // 2
+    copies = [pltpu.make_async_copy(refs[i], refs[count + i], refs[-1].at[i]) for i in range(count)]
+    for copy in copies:
+        copy.start()
+    for copy in copies:
+        copy.wait()
+
+
+def store_call(*arrays):
+    return pl.pallas_call(
+        store_kernel,
+        out_shape=tuple(jax.ShapeDtypeStruct(a.shape, a.dtype) for a in arrays),
+        in_specs=[pl.BlockSpec(memory_space=pltpu.VMEM)] * len(arrays),
+        out_specs=(pl.BlockSpec(memory_space=pltpu.HBM),) * len(arrays),
+        scratch_shapes=[pltpu.SemaphoreType.DMA((len(arrays),))],
+        compiler_params=pltpu.CompilerParams(vmem_limit_bytes=1024 * 1024),
+    )(*arrays)
+
+
+def pair_call(layer, n_tp, x, g, a, b, m, v):
     tokens, features = x.shape
     rows, width = g.shape
     model = a.shape[1]
     n_dp = 4
     cols = width // n_dp
-    lines = 8
     n_z = n_tp // 2
-    head = features // (HEADS + 2) * HEADS
+    chunks = features // LANES
+    span = model // 16
     dma = pltpu.SemaphoreType.DMA
     bf16, f32 = jnp.bfloat16, jnp.float32
     buffers = [
-        ((2, tokens, features), bf16), ((2, tokens, features - head), bf16),
-        ((n_dp, tokens, cols), bf16), ((2, tokens, cols), bf16),
-        ((head, cols), f32), ((head, cols), f32),
+        ((2, tokens, features), bf16), ((4, tokens, cols), bf16),
+        ((features, cols), bf16), ((features, cols), bf16), ((features, cols), f32),
+        ((features, cols), f32), ((features, cols), f32),
         ((rows, model), bf16), ((rows, model), bf16),
-        ((2, lines, model // lines), f32), ((n_z, lines, model // lines), f32), ((n_dp, lines, model // lines), f32),
+        ((2, 8, span), f32), ((2, 8, span), f32), ((2, 8, span), f32), ((2, 8, span), f32),
+        ((n_z, 8, span), f32), ((2, 8, span), f32),
     ]
+    total = jax.ShapeDtypeStruct((features, cols), f32)
     return pl.pallas_call(
-        functools.partial(square_kernel, n_tp),
-        out_shape=(
-            jax.ShapeDtypeStruct((features, cols), f32),
-            jax.ShapeDtypeStruct((model // 128, 128), f32),
+        functools.partial(pair_kernel, n_tp),
+        out_shape=(total, total, total, jax.ShapeDtypeStruct((model // LANES, LANES), f32)),
+        in_specs=[pl.BlockSpec(memory_space=pltpu.HBM)] * 6,
+        out_specs=(pl.BlockSpec(memory_space=pltpu.VMEM),) * 4,
+        scratch_shapes=[pltpu.VMEM(shape, dtype) for shape, dtype in buffers] + [
+            dma((7,)), dma((2,)), dma((2,)), dma((chunks,)), dma((chunks,)), dma((chunks, 2)), dma((chunks, 2)),
+        ] + [dma((5, n_z))] * 6 + [dma((4,)), dma((4,))],
+        compiler_params=pltpu.CompilerParams(
+            collective_id=layer, has_side_effects=True, vmem_limit_bytes=VMEM_LIMIT,
         ),
-        in_specs=[pl.BlockSpec(memory_space=pltpu.HBM)] * 4,
-        out_specs=(pl.BlockSpec(memory_space=pltpu.VMEM), pl.BlockSpec(memory_space=pltpu.VMEM)),
-        scratch_shapes=[pltpu.VMEM(shape, dtype) for shape, dtype in buffers] + [
-            dma((5,)), dma((HEADS,)), dma((HEADS,)), dma((3, 2)), dma((3, 2)), dma((2,)), dma((2,)),
-            dma((HEADS,)), dma((HEADS,)), dma((n_dp,)), dma((n_dp,)),
-        ] + [dma((4, n_z))] * 6 + [
-            dma((1,)), dma((1,)), dma((n_z,)), dma((n_z,)), dma((n_dp,)), dma((n_dp,)),
-        ],
-        compiler_params=pltpu.CompilerParams(
-            collective_id=layer, has_side_effects=True, vmem_limit_bytes=50 * 1024 * 1024,
-        ),
-    )(x, g, a, b)
+    )(x, g, a, b, m, v)
 
 
 def shards(n_dp, n_tp, proj_in, kv_grad, normed, norm_grad, first_moment, second_moment):
@@ -594,8 +633,11 @@
     n_z = n_tp // 2
     firsts, seconds, updates, gains = [], [], [], []
     for layer in range(layers):
-        if n_dp == 4 and features % (128 * (HEADS + 2)) == 0 and n_tp >= 6:
-            total, gain = square_call(layer, n_tp, proj_in[layer], kv_grad[layer], normed[layer], norm_grad[layer])
+        if n_dp == 4 and features % LANES == 0 and features >= 6 * LANES and model % (16 * LANES) == 0 and n_tp >= 6:
+            new_first, new_second, update, gain = store_call(*pair_call(
+                layer, n_tp, proj_in[layer], kv_grad[layer], normed[layer], norm_grad[layer],
+                first_moment[layer], second_moment[layer],
+            ))
         else:
             total, gain = pl.pallas_call(
                 functools.partial(kernel, n_dp, n_tp),
@@ -623,7 +665,7 @@
                     collective_id=layer, has_side_effects=True, vmem_limit_bytes=60 * 1024 * 1024,
                 ),
             )(proj_in[layer], kv_grad[layer], normed[layer], norm_grad[layer])
-        new_first, new_second, update = adam_update(total / n_dp, first_moment[layer], second_moment[layer])
+            new_first, new_second, update = adam_update(total / n_dp, first_moment[layer], second_moment[layer])
         firsts.append(new_first)
         seconds.append(new_second)
         updates.append(update)

time: 79.9 us -> 89.5 us (1.12)
  Pallas kernels: 73.8 us -> 87.7 us
  other arithmetic: 3.59 us -> 0 us
    pallas_call x1 -> x2, Pallas kernels: 73.8 us -> 87.7 us  [the longest x1 85 us: pair_call(): pl.pallas_call(functools.partial(pair_kernel, n_tp), out_shape=(total, to...]
    another operation x1 -> x0, other arithmetic: 3.59 us -> none  [shards(): jnp.stack(updates)]
where the time goes in v1:
time: 89.5 us; the launch traced here: 89.4 us
  Pallas kernels  87.7 us (98%)
  local copies, waits for them, and re-layouts  1.03 us (1%)
    pallas_call x1, Pallas kernels, pair_call(): pl.pallas_call(functools.partial(pair_kernel, n_tp), out_shape=(total, to...  85 us
    pallas_call x1, Pallas kernels, store_call(): pl.pallas_call(store_kernel, out_shape=tuple((jax.ShapeDtypeStruct(a.shap...  2.74 us

profile of v1, /device:TPU:0, one launch (start us, length us, event | category | flops | bytes accessed | tf_op | source)
XLA Modules:
  0.0 89.4 jit_solution(8543835408162619551)
XLA Ops:
  0.6 0.0 copy-start
  0.6 1.0 %copy-done = bf16[1,128,2048]{2,1,0:T(8,128)(2,1)S(1)} copy-done((bf16[1,128,2048]{2,1,0:T(8,128)(2,1)S(1)}, bf16[1,128,2048]{2,1,0:T(8,128)(2,1)}, u32[]{:S(2)}) %copy-start) | copy-done | bytes 524312
  1.7 85.0 %shard_map.93 = (f32[1024,512]{1,0:T(8,128)S(1)}, f32[1024,512]{1,0:T(8,128)S(1)}, f32[1024,512]{1,0:T(8,128)S(1)}, f32[64,128]{1,0:T(8,128)S(1)}) custom-call(bf16[1024,1024]{1,0:T(8,128)(2,1)} %bitcast.11, bf16[128,2048]{1,0:T(8,128)(2,1)S(1)} %bitcast.10, bf16[128,8192]{1,0:T(8,128)(2,1)} %bitcast.12, bf16[128,8192]{1,0:T(8,128)(2,1)} %bitcast.13, ...), custom_call_target="tpu_custom_call" | custom-call | tf_op jit(solution)/shard_map/pallas_call | solution.py:612
  86.6 2.7 %shard_map.94 = (f32[1024,512]{1,0:T(8,128)}, f32[1024,512]{1,0:T(8,128)}, f32[1024,512]{1,0:T(8,128)}, f32[64,128]{1,0:T(8,128)}) custom-call(f32[1024,512]{1,0:T(8,128)S(1)} %get-tuple-element.12.refs_0_, f32[1024,512]{1,0:T(8,128)S(1)} %get-tuple-element.13.refs_1_, f32[1024,512]{1,0:T(8,128)S(1)} %get-tuple-element.14.refs_2_, ...), custom_call_target="tpu_custom_call" | custom-call | tf_op jit(solution)/shard_map/pallas_call | solution.py:582
Async XLA Ops:
  0.6 1.0 %copy-start = (bf16[1,128,2048]{2,1,0:T(8,128)(2,1)S(1)}, bf16[1,128,2048]{2,1,0:T(8,128)(2,1)}, u32[]{:S(2)}) copy-start(bf16[1,128,2048]{2,1,0:T(8,128)(2,1)} %param.7) | copy-start | bytes 1572868

commit v2 on v1

--- a/solution.py
+++ b/solution.py
@@ -17,6 +17,7 @@
 LANES = 128
 SPAN = 250.0
 KNEE = 2.0 ** -5
+EARLY = 2
 VMEM_LIMIT = 46 * 1024 * 1024
 
 
@@ -362,7 +363,7 @@
 
     go(swaps[0])
     go(swaps[1])
-    for k in range(chunks):
+    for k in range(EARLY):
         go(x_copy(k))
 
     GAIN = 4
@@ -482,17 +483,22 @@
             at = pl.ds((h * lines + j) * span, span)
             products = a_buf[:, at].astype(jnp.float32) * b_buf[:, at].astype(jnp.float32)
             gain_half[h, pl.ds(j, 1), :] = jnp.sum(products, axis=0, keepdims=True)
-    go(gain_copy(0, gain_half.at[1 - core], gain_pair.at[1], {"tp": other}))
+    pair_gain = gain_copy(0, gain_half.at[1 - core], gain_pair.at[1], {"tp": other})
+    beside_gain = gain_copy(1, gain_x.at[0], gain_x.at[1], {"dp": beside})
+    across_gain = gain_copy(2, gain_y.at[0], gain_y.at[1], {"dp": across})
+    go(pair_gain)
     swaps[0].wait_recv()
     chain(1, 1)
+    pair_gain.wait_recv()
+    gain_x[0] = gain_half[core] + gain_pair[1]
+    go(beside_gain)
+    for k in range(EARLY, chunks):
+        go(x_copy(k))
     chain(0, 2)
-    gain_copy(0, gain_half.at[1 - core], gain_pair.at[1], {"tp": other}).wait_recv()
-    gain_x[0] = gain_half[core] + gain_pair[1]
-    go(gain_copy(1, gain_x.at[0], gain_x.at[1], {"dp": beside}))
+    swaps[1].wait_recv()
     chain(1, 2)
     chain(0, 3)
     chain(1, 3)
-    swaps[1].wait_recv()
     chain(3, 1)
     chain(2, 2)
     for s in range(4, n_z + 1):
@@ -503,52 +509,57 @@
     locals_[4].wait()
 
     partial(0)
-    gain_copy(1, gain_x.at[0], gain_x.at[1], {"dp": beside}).wait_recv()
+    chain(3, 2)
+    partial(1)
+    chain(2, 3)
+    beside_gain.wait_recv()
     gain_y[0] = gain_x[0] + gain_x[1]
-    go(gain_copy(2, gain_y.at[0], gain_y.at[1], {"dp": across}))
-    chain(3, 2)
-    chain(2, 3)
-    partial(1)
-    gain_copy(2, gain_y.at[0], gain_y.at[1], {"dp": across}).wait_recv()
+    go(across_gain)
+    chain(3, 3)
+    partial(2)
+    across_gain.wait_recv()
     gain_z[z] = gain_y[0] + gain_y[1]
     chain(GAIN, 1)
-    chain(3, 3)
-    partial(2)
-    chain(GAIN, 2)
+    partial(3)
     for s in range(4, n_z + 1):
         chain(2, s)
+    partial(4)
+    for s in range(4, n_z + 1):
         chain(3, s)
-    partial(3)
-    for s in range(3, n_z + 1):
-        chain(GAIN, s)
+    chain(GAIN, 2)
     complete(2)
     complete(3)
-    own_sum(0)
-    own_sum(1)
-    gain_all[core] = jnp.sum(gain_z[...], axis=0) / n_dp
-    go(gain_copy(3, gain_all.at[core], gain_all.at[core], {"tp": other}))
     for copy in locals_[5:]:
         copy.wait()
-    finish(0)
-    done, finished = 2, 1
-    for k in range(4, chunks):
-        partial(k)
-        while done < k:
+    for k in range(3):
+        own_sum(k)
+    for k in range(2):
+        finish(k)
+    partial(5)
+    chain(GAIN, 3)
+    done, finished = 3, 2
+    for k in range(6, chunks):
+        while done < k - 1:
             own_sum(done)
             done += 1
             if finished < done - 1:
                 finish(finished)
                 finished += 1
-        if k == 4:
-            gain_copy(3, gain_all.at[1 - core], gain_all.at[1 - core], {"tp": other}).wait_recv()
-            per = span // LANES
-            for h in range(2):
-                for i in range(per):
-                    at = pl.ds(h * lines * per + i, lines, stride=per)
-                    gain_ref[at, :] = gain_all[h, :, i * LANES:(i + 1) * LANES]
+        partial(k)
+        if k == 6:
+            for s in range(4, n_z + 1):
+                chain(GAIN, s)
+            gain_all[core] = jnp.sum(gain_z[...], axis=0) / n_dp
+            go(gain_copy(3, gain_all.at[core], gain_all.at[core], {"tp": other}))
     while done < chunks:
         own_sum(done)
         done += 1
+    gain_copy(3, gain_all.at[1 - core], gain_all.at[1 - core], {"tp": other}).wait_recv()
+    per = span // LANES
+    for h in range(2):
+        for i in range(per):
+            at = pl.ds(h * lines * per + i, lines, stride=per)
+            gain_ref[at, :] = gain_all[h, :, i * LANES:(i + 1) * LANES]
     while finished < chunks:
         finish(finished)
         finished += 1
@@ -633,7 +644,7 @@
     n_z = n_tp // 2
     firsts, seconds, updates, gains = [], [], [], []
     for layer in range(layers):
-        if n_dp == 4 and features % LANES == 0 and features >= 6 * LANES and model % (16 * LANES) == 0 and n_tp >= 6:
+        if n_dp == 4 and features % LANES == 0 and features >= 8 * LANES and model % (16 * LANES) == 0 and n_tp >= 6:
             new_first, new_second, update, gain = store_call(*pair_call(
                 layer, n_tp, proj_in[layer], kv_grad[layer], normed[layer], norm_grad[layer],
                 first_moment[layer], second_moment[layer],

time: 89.5 us -> 67.4 us (0.75)
  Pallas kernels: 87.7 us -> 65.5 us
    pallas_call x1, Pallas kernels: 85 us -> 62.8 us  [pair_call(): pl.pallas_call(functools.partial(pair_kernel, n_tp), out_shape=(total, to...]
where the time goes in v2:
time: 67.4 us; the launch traced here: 67.2 us
  Pallas kernels  65.5 us (97%)
  local copies, waits for them, and re-layouts  1.03 us (2%)
    pallas_call x1, Pallas kernels, pair_call(): pl.pallas_call(functools.partial(pair_kernel, n_tp), out_shape=(total, to...  62.8 us
    pallas_call x1, Pallas kernels, store_call(): pl.pallas_call(store_kernel, out_shape=tuple((jax.ShapeDtypeStruct(a.shap...  2.74 us

profile of v2, /device:TPU:0, one launch (start us, length us, event | category | flops | bytes accessed | tf_op | source)
XLA Modules:
  0.0 67.2 jit_solution(7236528064252877695)
XLA Ops:
  0.6 0.0 copy-start
  0.6 1.0 %copy-done = bf16[1,128,2048]{2,1,0:T(8,128)(2,1)S(1)} copy-done((bf16[1,128,2048]{2,1,0:T(8,128)(2,1)S(1)}, bf16[1,128,2048]{2,1,0:T(8,128)(2,1)}, u32[]{:S(2)}) %copy-start) | copy-done | bytes 524312
  1.7 62.8 %shard_map.93 = (f32[1024,512]{1,0:T(8,128)S(1)}, f32[1024,512]{1,0:T(8,128)S(1)}, f32[1024,512]{1,0:T(8,128)S(1)}, f32[64,128]{1,0:T(8,128)S(1)}) custom-call(bf16[1024,1024]{1,0:T(8,128)(2,1)} %bitcast.11, bf16[128,2048]{1,0:T(8,128)(2,1)S(1)} %bitcast.10, bf16[128,8192]{1,0:T(8,128)(2,1)} %bitcast.12, bf16[128,8192]{1,0:T(8,128)(2,1)} %bitcast.13, ...), custom_call_target="tpu_custom_call" | custom-call | tf_op jit(solution)/shard_map/pallas_call | solution.py:623
  64.5 2.7 %shard_map.94 = (f32[1024,512]{1,0:T(8,128)}, f32[1024,512]{1,0:T(8,128)}, f32[1024,512]{1,0:T(8,128)}, f32[64,128]{1,0:T(8,128)}) custom-call(f32[1024,512]{1,0:T(8,128)S(1)} %get-tuple-element.12.refs_0_, f32[1024,512]{1,0:T(8,128)S(1)} %get-tuple-element.13.refs_1_, f32[1024,512]{1,0:T(8,128)S(1)} %get-tuple-element.14.refs_2_, ...), custom_call_target="tpu_custom_call" | custom-call | tf_op jit(solution)/shard_map/pallas_call | solution.py:593
Async XLA Ops:
  0.6 1.0 %copy-start = (bf16[1,128,2048]{2,1,0:T(8,128)(2,1)S(1)}, bf16[1,128,2048]{2,1,0:T(8,128)(2,1)}, u32[]{:S(2)}) copy-start(bf16[1,128,2048]{2,1,0:T(8,128)(2,1)} %param.7) | copy-start | bytes 1572868

commit v3 on v2

--- a/solution.py
+++ b/solution.py
@@ -288,7 +288,7 @@
     n_tp, x_hbm, g_hbm, a_hbm, b_hbm, m_hbm, v_hbm, first_ref, second_ref, step_ref, gain_ref,
     xs, kv, part, arrived, own, m_buf, v_buf, a_buf, b_buf, gain_half, gain_pair, gain_x, gain_y, gain_z, gain_all,
     local_sem, swap_send, swap_recv, x_send, x_recv, part_send, part_recv,
-    up_send, up_recv, down_send, down_recv, pair_send, pair_recv, gain_send, gain_recv,
+    up_send, up_recv, down_send, down_recv, pair_send, pair_recv, gain_send, gain_recv, upper_in, ready,
 ):
     n_dp = 4
     dp = lax.axis_index("dp")
@@ -346,11 +346,11 @@
     def _():
         hello({"tp": tp + 2})
 
+    pl.semaphore_wait(barrier, 3 + jnp.where(z >= 1, 1, 0))
+
     @pl.when(z >= 1)
     def _():
-        hello({"tp": tp - 2})
-
-    pl.semaphore_wait(barrier, 3 + jnp.where(z + 1 < n_z, 1, 0) + jnp.where(z >= 1, 1, 0))
+        pl.semaphore_signal(upper_in, inc=1, device_id={"tp": tp - 2}, device_id_type=pl.DeviceIdType.MESH)
 
     def swap(i, plane, d):
         return remote(g_cols(d), kv.at[plane, my_rows, :], swap_send.at[i], swap_recv.at[i], {"dp": beside})
@@ -448,10 +448,14 @@
 
     def partial(k):
         at = pl.ds(k * LANES, LANES)
+        last = k == chunks - 1
+        if last:
+            ready[...] = dot(xs[0, :, at], kv[0])
         x_copy(k).wait_recv()
         for h in range(halves):
             ch = pl.ds(h * wide, wide)
-            total = dot(xs[0, :, at], kv[0, :, ch]) + dot(xs[1, :, at], kv[1, :, ch])
+            head = ready[:, ch] if last else dot(xs[0, :, at], kv[0, :, ch])
+            total = head + dot(xs[1, :, at], kv[1, :, ch])
             part[at, ch] = encode(total, bound)
             go(part_copy(k, h))
 
@@ -469,6 +473,10 @@
             first_ref[at, ch] = new_first
             second_ref[at, ch] = new_second
             step_ref[at, ch] = update
+
+    @pl.when(z + 1 < n_z)
+    def _():
+        pl.semaphore_wait(upper_in, 1)
 
     locals_[0].wait()
     chain(0, 1)
@@ -537,32 +545,31 @@
         finish(k)
     partial(5)
     chain(GAIN, 3)
-    done, finished = 3, 2
-    for k in range(6, chunks):
-        while done < k - 1:
-            own_sum(done)
-            done += 1
-            if finished < done - 1:
-                finish(finished)
-                finished += 1
-        partial(k)
-        if k == 6:
-            for s in range(4, n_z + 1):
-                chain(GAIN, s)
-            gain_all[core] = jnp.sum(gain_z[...], axis=0) / n_dp
-            go(gain_copy(3, gain_all.at[core], gain_all.at[core], {"tp": other}))
-    while done < chunks:
-        own_sum(done)
-        done += 1
+    for k in range(3, 6):
+        own_sum(k)
+    for k in range(2, 5):
+        finish(k)
+    partial(6)
+    for s in range(4, n_z + 1):
+        chain(GAIN, s)
+    gain_all[core] = jnp.sum(gain_z[...], axis=0) / n_dp
+    last_gain = gain_copy(3, gain_all.at[core], gain_all.at[core], {"tp": other})
+    go(last_gain)
+    own_sum(6)
+    finish(5)
     gain_copy(3, gain_all.at[1 - core], gain_all.at[1 - core], {"tp": other}).wait_recv()
     per = span // LANES
     for h in range(2):
         for i in range(per):
             at = pl.ds(h * lines * per + i, lines, stride=per)
             gain_ref[at, :] = gain_all[h, :, i * LANES:(i + 1) * LANES]
-    while finished < chunks:
-        finish(finished)
-        finished += 1
+    finish(6)
+    for k in range(7, chunks):
+        partial(k)
+    for k in range(7, chunks):
+        own_sum(k)
+    for k in range(7, chunks):
+        finish(k)
 
     for copy in sent:
         copy.wait_send()
@@ -627,7 +634,7 @@
         out_specs=(pl.BlockSpec(memory_space=pltpu.VMEM),) * 4,
         scratch_shapes=[pltpu.VMEM(shape, dtype) for shape, dtype in buffers] + [
             dma((7,)), dma((2,)), dma((2,)), dma((chunks,)), dma((chunks,)), dma((chunks, 2)), dma((chunks, 2)),
-        ] + [dma((5, n_z))] * 6 + [dma((4,)), dma((4,))],
+        ] + [dma((5, n_z))] * 6 + [dma((4,)), dma((4,)), pltpu.SemaphoreType.REGULAR, pltpu.VMEM((LANES, cols), f32)],
         compiler_params=pltpu.CompilerParams(
             collective_id=layer, has_side_effects=True, vmem_limit_bytes=VMEM_LIMIT,
         ),
@@ -646,7 +653,7 @@
     for layer in range(layers):
         if n_dp == 4 and features % LANES == 0 and features >= 8 * LANES and model % (16 * LANES) == 0 and n_tp >= 6:
             new_first, new_second, update, gain = store_call(*pair_call(
-                layer, n_tp, proj_in[layer], kv_grad[layer], normed[layer], norm_grad[layer],
+                layer, n_tp, proj_in[layer], pltpu.with_memory_space_constraint(kv_grad[layer], pltpu.HBM), normed[layer], norm_grad[layer],
                 first_moment[layer], second_moment[layer],
             ))
         else:

time: 67.4 us -> 66.1 us (0.981)
  local copies, waits for them, and re-layouts: 1.03 us -> 0 us
    unnamed x2 -> x0, local copies, waits for them, and re-layouts: 1.03 us -> none
where the time goes in v3:
time: 66.1 us; the launch traced here: 66 us
  Pallas kernels  65.3 us (99%)
    pallas_call x1, Pallas kernels, pair_call(): pl.pallas_call(functools.partial(pair_kernel, n_tp), out_shape=(total, to...  62.6 us
    pallas_call x1, Pallas kernels, store_call(): pl.pallas_call(store_kernel, out_shape=tuple((jax.ShapeDtypeStruct(a.shap...  2.74 us

profile of v3, /device:TPU:0, one launch (start us, length us, event | category | flops | bytes accessed | tf_op | source)
XLA Modules:
  0.0 66.0 jit_solution(13807506849405462385)
XLA Ops:
  0.6 62.6 %shard_map.93 = (f32[1024,512]{1,0:T(8,128)S(1)}, f32[1024,512]{1,0:T(8,128)S(1)}, f32[1024,512]{1,0:T(8,128)S(1)}, f32[64,128]{1,0:T(8,128)S(1)}) custom-call(bf16[1024,1024]{1,0:T(8,128)(2,1)} %bitcast.10, bf16[128,2048]{1,0:T(8,128)(2,1)} %bitcast.15, bf16[128,8192]{1,0:T(8,128)(2,1)} %bitcast.11, bf16[128,8192]{1,0:T(8,128)(2,1)} %bitcast.12, ...), custom_call_target="tpu_custom_call" | custom-call | tf_op jit(solution)/shard_map/pallas_call | solution.py:630
  63.2 2.7 %shard_map.94 = (f32[1024,512]{1,0:T(8,128)}, f32[1024,512]{1,0:T(8,128)}, f32[1024,512]{1,0:T(8,128)}, f32[64,128]{1,0:T(8,128)}) custom-call(f32[1024,512]{1,0:T(8,128)S(1)} %get-tuple-element.12.refs_0_, f32[1024,512]{1,0:T(8,128)S(1)} %get-tuple-element.13.refs_1_, f32[1024,512]{1,0:T(8,128)S(1)} %get-tuple-element.14.refs_2_, ...), custom_call_target="tpu_custom_call" | custom-call | tf_op jit(solution)/shard_map/pallas_call | solution.py:600

commit v4 on v3

--- a/solution.py
+++ b/solution.py
@@ -16,7 +16,10 @@
 PIECES = 4
 LANES = 128
 SPAN = 250.0
-KNEE = 2.0 ** -5
+KNEE = 2.0 ** -10
+POWER = SPAN / math.log2(1.0 + 1.0 / KNEE)
+TINY = 2.0 ** -100
+NOTE = 16
 EARLY = 2
 VMEM_LIMIT = 46 * 1024 * 1024
 
@@ -271,16 +274,18 @@
         to_pair(b).wait_send()
 
 
-def encode(value, bound):
-    power = SPAN / math.log2(1.0 + bound / KNEE)
-    code = jnp.exp2(power * jnp.log2(1.0 + jnp.abs(value) * (1.0 / KNEE)) - SPAN / 2)
+def scale_of(held):
+    return jnp.maximum(held.astype(jnp.float32), TINY)
+
+
+def encode(value, scale):
+    code = jnp.exp2(POWER * jnp.log2(1.0 + jnp.abs(value) * (1.0 / (scale * KNEE))) - SPAN / 2)
     return jnp.where(value < 0.0, -code, code).astype(jnp.bfloat16)
 
 
-def decode(code, bound):
-    power = SPAN / math.log2(1.0 + bound / KNEE)
+def decode(code, scale):
     code = code.astype(jnp.float32)
-    value = (jnp.exp2((jnp.log2(jnp.abs(code)) + SPAN / 2) * (1.0 / power)) - 1.0) * KNEE
+    value = (jnp.exp2((jnp.log2(jnp.abs(code)) + SPAN / 2) * (1.0 / POWER)) - 1.0) * (scale * KNEE)
     return jnp.where(code < 0.0, -value, value)
 
 
@@ -300,7 +305,6 @@
     cols = kv.shape[2]
     tokens, features = x_hbm.shape
     chunks = features // LANES
-    bound = 2.0 * tokens * 6.0 * 0.75
     other = 2 * z + 1 - core
     beside = jnp.bitwise_xor(dp, 1)
     across = jnp.bitwise_xor(dp, 2)
@@ -443,7 +447,7 @@
     wide = cols // halves
 
     def part_copy(k, h):
-        at = (pl.ds(k * LANES, LANES), pl.ds(h * wide, wide))
+        at = (k, slice(None), pl.ds(h * wide, wide))
         return remote(part.at[at], arrived.at[at], part_send.at[k, h], part_recv.at[k, h], {"dp": across})
 
     def partial(k):
@@ -456,7 +460,9 @@
             ch = pl.ds(h * wide, wide)
             head = ready[:, ch] if last else dot(xs[0, :, at], kv[0, :, ch])
             total = head + dot(xs[1, :, at], kv[1, :, ch])
-            part[at, ch] = encode(total, bound)
+            held = jnp.max(jnp.abs(total), axis=0, keepdims=True).astype(jnp.bfloat16)
+            part[k, pl.ds(LANES, NOTE), ch] = jnp.broadcast_to(held, (NOTE, wide))
+            part[k, pl.ds(0, LANES), ch] = encode(total, scale_of(held))
             go(part_copy(k, h))
 
     def own_sum(k):
@@ -468,7 +474,8 @@
         for h in range(halves):
             ch = pl.ds(h * wide, wide)
             part_copy(k, h).wait_recv()
-            mean = (own[at, ch] + decode(arrived[at, ch], bound)) / n_dp
+            scale = scale_of(arrived[k, pl.ds(LANES, NOTE), ch][:1])
+            mean = (own[at, ch] + decode(arrived[k, pl.ds(0, LANES), ch], scale)) / n_dp
             new_first, new_second, update = adam_update(mean, m_buf[at, ch], v_buf[at, ch])
             first_ref[at, ch] = new_first
             second_ref[at, ch] = new_second
@@ -620,7 +627,7 @@
     bf16, f32 = jnp.bfloat16, jnp.float32
     buffers = [
         ((2, tokens, features), bf16), ((4, tokens, cols), bf16),
-        ((features, cols), bf16), ((features, cols), bf16), ((features, cols), f32),
+        ((chunks, LANES + NOTE, cols), bf16), ((chunks, LANES + NOTE, cols), bf16), ((features, cols), f32),
         ((features, cols), f32), ((features, cols), f32),
         ((rows, model), bf16), ((rows, model), bf16),
         ((2, 8, span), f32), ((2, 8, span), f32), ((2, 8, span), f32), ((2, 8, span), f32),

time: 66.1 us -> 66.6 us (level)
  no operation moved by 1% of the time
where the time goes in v4:
time: 66.6 us; the launch traced here: 66.4 us
  Pallas kernels  65.8 us (99%)
    pallas_call x1, Pallas kernels, pair_call(): pl.pallas_call(functools.partial(pair_kernel, n_tp), out_shape=(total, to...  63 us
    pallas_call x1, Pallas kernels, store_call(): pl.pallas_call(store_kernel, out_shape=tuple((jax.ShapeDtypeStruct(a.shap...  2.74 us

profile of v4, /device:TPU:0, one launch (start us, length us, event | category | flops | bytes accessed | tf_op | source)
XLA Modules:
  0.0 66.4 jit_solution(12385632433734403999)
XLA Ops:
  0.6 63.0 %shard_map.93 = (f32[1024,512]{1,0:T(8,128)S(1)}, f32[1024,512]{1,0:T(8,128)S(1)}, f32[1024,512]{1,0:T(8,128)S(1)}, f32[64,128]{1,0:T(8,128)S(1)}) custom-call(bf16[1024,1024]{1,0:T(8,128)(2,1)} %bitcast.10, bf16[128,2048]{1,0:T(8,128)(2,1)} %bitcast.15, bf16[128,8192]{1,0:T(8,128)(2,1)} %bitcast.11, bf16[128,8192]{1,0:T(8,128)(2,1)} %bitcast.12, ...), custom_call_target="tpu_custom_call" | custom-call | tf_op jit(solution)/shard_map/pallas_call | solution.py:637
  63.7 2.7 %shard_map.94 = (f32[1024,512]{1,0:T(8,128)}, f32[1024,512]{1,0:T(8,128)}, f32[1024,512]{1,0:T(8,128)}, f32[64,128]{1,0:T(8,128)}) custom-call(f32[1024,512]{1,0:T(8,128)S(1)} %get-tuple-element.12.refs_0_, f32[1024,512]{1,0:T(8,128)S(1)} %get-tuple-element.13.refs_1_, f32[1024,512]{1,0:T(8,128)S(1)} %get-tuple-element.14.refs_2_, ...), custom_call_target="tpu_custom_call" | custom-call | tf_op jit(solution)/shard_map/pallas_call | solution.py:607

commit v5 on v4

--- a/solution.py
+++ b/solution.py
@@ -505,8 +505,8 @@
     swaps[0].wait_recv()
     chain(1, 1)
     pair_gain.wait_recv()
-    gain_x[0] = gain_half[core] + gain_pair[1]
-    go(beside_gain)
+    gain_y[0] = gain_half[core] + gain_pair[1]
+    go(across_gain)
     for k in range(EARLY, chunks):
         go(x_copy(k))
     chain(0, 2)
@@ -527,9 +527,6 @@
     chain(3, 2)
     partial(1)
     chain(2, 3)
-    beside_gain.wait_recv()
-    gain_y[0] = gain_x[0] + gain_x[1]
-    go(across_gain)
     chain(3, 3)
     partial(2)
     across_gain.wait_recv()
@@ -559,22 +556,24 @@
     partial(6)
     for s in range(4, n_z + 1):
         chain(GAIN, s)
-    gain_all[core] = jnp.sum(gain_z[...], axis=0) / n_dp
-    last_gain = gain_copy(3, gain_all.at[core], gain_all.at[core], {"tp": other})
-    go(last_gain)
+    gain_x[0] = jnp.sum(gain_z[...], axis=0)
+    go(beside_gain)
     own_sum(6)
     finish(5)
+    finish(6)
+    for k in range(7, chunks):
+        partial(k)
+    for k in range(7, chunks):
+        own_sum(k)
+    beside_gain.wait_recv()
+    gain_all[core] = (gain_x[0] + gain_x[1]) / n_dp
+    go(gain_copy(3, gain_all.at[core], gain_all.at[core], {"tp": other}))
     gain_copy(3, gain_all.at[1 - core], gain_all.at[1 - core], {"tp": other}).wait_recv()
     per = span // LANES
     for h in range(2):
         for i in range(per):
             at = pl.ds(h * lines * per + i, lines, stride=per)
             gain_ref[at, :] = gain_all[h, :, i * LANES:(i + 1) * LANES]
-    finish(6)
-    for k in range(7, chunks):
-        partial(k)
-    for k in range(7, chunks):
-        own_sum(k)
     for k in range(7, chunks):
         finish(k)
 

time: 66.6 us -> 66.2 us (level)
  no operation moved by 1% of the time
where the time goes in v5:
time: 66.2 us; the launch traced here: 66.1 us
  Pallas kernels  65.4 us (99%)
    pallas_call x1, Pallas kernels, pair_call(): pl.pallas_call(functools.partial(pair_kernel, n_tp), out_shape=(total, to...  62.7 us
    pallas_call x1, Pallas kernels, store_call(): pl.pallas_call(store_kernel, out_shape=tuple((jax.ShapeDtypeStruct(a.shap...  2.74 us

profile of v5, /device:TPU:0, one launch (start us, length us, event | category | flops | bytes accessed | tf_op | source)
XLA Modules:
  0.0 66.1 jit_solution(13100465615529925366)
XLA Ops:
  0.6 62.7 %shard_map.93 = (f32[1024,512]{1,0:T(8,128)S(1)}, f32[1024,512]{1,0:T(8,128)S(1)}, f32[1024,512]{1,0:T(8,128)S(1)}, f32[64,128]{1,0:T(8,128)S(1)}) custom-call(bf16[1024,1024]{1,0:T(8,128)(2,1)} %bitcast.10, bf16[128,2048]{1,0:T(8,128)(2,1)} %bitcast.15, bf16[128,8192]{1,0:T(8,128)(2,1)} %bitcast.11, bf16[128,8192]{1,0:T(8,128)(2,1)} %bitcast.12, ...), custom_call_target="tpu_custom_call" | custom-call | tf_op jit(solution)/shard_map/pallas_call | solution.py:636
  63.3 2.7 %shard_map.94 = (f32[1024,512]{1,0:T(8,128)}, f32[1024,512]{1,0:T(8,128)}, f32[1024,512]{1,0:T(8,128)}, f32[64,128]{1,0:T(8,128)}) custom-call(f32[1024,512]{1,0:T(8,128)S(1)} %get-tuple-element.12.refs_0_, f32[1024,512]{1,0:T(8,128)S(1)} %get-tuple-element.13.refs_1_, f32[1024,512]{1,0:T(8,128)S(1)} %get-tuple-element.14.refs_2_, ...), custom_call_target="tpu_custom_call" | custom-call | tf_op jit(solution)/shard_map/pallas_call | solution.py:606
